TPU v7x, 32 devices: a whole 2x2x4 slice. The times are simulated.
32 devices in a mesh: groups: 2 (over y), owners: 4 (over x, core), sub: 4 (over z).
Axes of the slice: x: 2, y: 2, z: 4, core: 2. Of those that a mesh axis runs over, the one named last changes fastest.
Arguments:
- embeddings: bfloat16 [16384, 768], P(('groups', 'owners', 'sub')), parts along dimension 0, may hold values from -6 to 6, as said below
- class_table: bfloat16 [1000, 768], replicated, may hold values from -6 to 6
- nearest: int32 [16384], P(('groups', 'owners', 'sub')), parts along dimension 0, may hold values from 0 to 999
- keep_class: int32 [1000], replicated, may hold values 0 or 1
- destination: int32 [16384, 1], P(('groups', 'owners', 'sub')), parts along dimension 0, may hold values from 0 to 15; in each aligned block of 512 rows (0 to 511, 512 to 1023, ...) at most 48 rows name the same one
Outputs:
- received_rows: bfloat16 [24576, 768], P(('groups', 'owners', 'sub')), parts along dimension 0
- received_score: bfloat16 [24576], P(('groups', 'owners', 'sub')), parts along dimension 0
- received_position: int32 [24576], P(('groups', 'owners', 'sub')), parts along dimension 0
- shard_totals: int32 [32], P('groups'), parts along dimension 0
There are 2 independent parts, one for each index of `groups`. A program takes and returns all parts, laid end to end along the dimension named above; an argument that names none is the same for every part. Nothing has to cross between parts.
Inputs may be any that keep to these rules, and one draw needn't show every extreme that they name: `destination`: in the rows of one device no loader shard is named by more than 48 rows. Counts of rows per loader shard may be packed several to an int32 word wherever they travel; this is an exception to the 4-bit rule below. `embeddings`: some rows are entirely zero.
All inputs are finite; a program needn't handle non-finite values.
Results may differ from a plain program's by a relative error of at most 0.001.
Values may be sent and summed in bfloat16 or wider, within the bound.
A program may use at most 64 MiB of HBM per device.

v0:
```python
import functools

import jax
import jax.numpy as jnp
from jax import lax
from jax.experimental import pallas as pl
from jax.experimental.pallas import tpu as pltpu
from jax.sharding import PartitionSpec as P

MESH = pl.DeviceIdType.MESH
CROSS = (((1,), (1,)), ((), ()))
DOWN = (((0,), (0,)), ((), ()))


def up(value, step):
    return (value + step - 1) // step * step


def place(owners, subs, k):
    o, z = lax.axis_index("owners"), lax.axis_index("sub")
    upper = (2 * z) // subs
    toward = upper * z + (1 - upper) * (subs - 1 - z)
    j = k // owners
    first = 1 - (j + subs - 1) // subs
    past = (j + subs - toward) // subs
    far = first * toward + (1 - first) * (j + past)
    to_sub = (z + far * (1 - 2 * upper) + subs) % subs
    to_owner = (o + 1 + k % owners) % owners
    return to_owner, to_sub


def finish_kernel(rows_ref, score_ref, position_ref, totals_ref, rows_out, score_out, position_out, totals_out,
                  score_s, position_s, totals_s, sem):
    copies = [pltpu.make_async_copy(rows_ref, rows_out, sem.at[0])]
    copies[0].start()
    position_s[...] = position_ref[...].reshape(position_s.shape)
    totals_s[...] = totals_ref[...].reshape(totals_s.shape)
    score_s[...] = score_ref[...].reshape(score_s.shape).astype(score_s.dtype)
    for i, (inner, outer) in enumerate(((position_s, position_out), (totals_s, totals_out), (score_s, score_out))):
        copies.append(pltpu.make_async_copy(inner, outer, sem.at[i + 1]))
        copies[-1].start()
    for copy in copies:
        copy.wait()


def kernel(owners, subs, cap, early, near_hbm, keep_hbm, dest_hbm, emb_hbm, table_hbm,
           rows_ref, score_ref, position_ref, totals_ref,
           near_ref, keep_ref, dest_ref, emb, table, keep2, send, meta, got, spots, counts_s, scores_s, slot_s,
           in_sem, send_sem, recv_sem, meta_send, meta_recv, own_sem):
    f32, bf16, i32 = jnp.float32, jnp.bfloat16, jnp.int32
    shards = owners * subs
    rows, width = emb.shape
    classes = table.shape[0]
    wide = meta.shape[2]
    slots = shards * cap
    o, z = lax.axis_index("owners"), lax.axis_index("sub")
    own = o * subs + z

    small = [
        pltpu.make_async_copy(near_hbm, near_ref, in_sem.at[2]),
        pltpu.make_async_copy(keep_hbm, keep_ref, in_sem.at[3]),
        pltpu.make_async_copy(dest_hbm, dest_ref, in_sem.at[4]),
    ]
    for copy in small:
        copy.start()
    emb_copy = pltpu.make_async_copy(emb_hbm, emb, in_sem.at[0])
    emb_copy.start()
    table_copy = pltpu.make_async_copy(table_hbm, table, in_sem.at[1])
    table_copy.start()

    barrier = pltpu.get_barrier_semaphore()

    def greet(k, c):
        a, b = place(owners, subs, k)
        pl.semaphore_signal(barrier, inc=1, device_id={"owners": a, "sub": b}, device_id_type=MESH)
        return c

    lax.fori_loop(0, shards - 1, greet, 0)

    for copy in small:
        copy.wait()
    near = near_ref[...]
    target = dest_ref[...]
    keep2[...] = jnp.zeros_like(keep2)
    for h in range(up(classes, 128) // 128):
        n = min(128, classes - h * 128)
        keep2[h : h + 1, :n] = keep_ref[:, h * 128 : h * 128 + n].astype(f32)
    deep = keep2.shape[0]
    high = near // 128
    low = near - high * 128
    low_hot = (lax.broadcasted_iota(i32, (128, rows), 0) == low).astype(f32).astype(bf16)
    by_high = jnp.dot(keep2[...].astype(bf16), low_hot, preferred_element_type=f32)
    kept = jnp.sum(
        jnp.where(lax.broadcasted_iota(i32, (deep, rows), 0) == high, by_high, 0.0), axis=0, keepdims=True
    )
    shard_hot = jnp.where(lax.broadcasted_iota(i32, (wide, rows), 0) == target, kept, 0.0)
    shard_bf = shard_hot.astype(bf16)
    earlier = (
        lax.broadcasted_iota(i32, (rows, rows), 0) < lax.broadcasted_iota(i32, (rows, rows), 1)
    ).astype(f32).astype(bf16)
    running = jnp.dot(shard_bf, earlier, preferred_element_type=f32)
    rank = jnp.sum(shard_hot * running, axis=0, keepdims=True).astype(i32)
    slot_s[...] = jnp.where(kept > 0.5, target * cap + rank, -1)

    emb_copy.wait()

    def fill(k):
        a, b = place(owners, subs, k)
        t = a * subs + b
        hot = (slot_s[...] == t * cap + lax.broadcasted_iota(i32, (cap, rows), 0)).astype(f32).astype(bf16)
        send[k] = jnp.dot(hot, emb[...], preferred_element_type=f32).astype(bf16)

    def row_copy(k, source):
        a, b = place(owners, subs, k)
        return pltpu.make_async_remote_copy(
            src_ref=send.at[k], dst_ref=rows_ref.at[source],
            send_sem=send_sem.at[k], recv_sem=recv_sem.at[source],
            device_id={"owners": a, "sub": b}, device_id_type=MESH,
        )

    def meta_copy(k, source):
        a, b = place(owners, subs, k)
        return pltpu.make_async_remote_copy(
            src_ref=meta.at[k], dst_ref=got.at[source],
            send_sem=meta_send.at[k], recv_sem=meta_recv.at[source],
            device_id={"owners": a, "sub": b}, device_id_type=MESH,
        )

    def step(k, c):
        fill(k)
        row_copy(k - 1, own).start()
        return c

    fill(0)
    fill(1)
    pl.semaphore_wait(barrier, shards - 1)
    row_copy(0, own).start()
    lax.fori_loop(2, early, step, 0)

    square = emb[...].astype(f32)
    square = square * square
    square_hi = square.astype(bf16)
    square_lo = (square - square_hi.astype(f32)).astype(bf16)
    ones = jnp.ones((8, width), bf16)
    total = lax.dot_general(ones, square_hi, CROSS, preferred_element_type=f32)
    total = total + lax.dot_general(ones, square_lo, CROSS, preferred_element_type=f32)
    inverse_row = lax.rsqrt(total[0:1] + 1e-06)
    table_copy.wait()
    given = jnp.zeros((1, rows), f32)
    others = jnp.full((1, rows), -1e30, f32)
    for lo in range(0, classes, 128):
        n = min(128, classes - lo)
        part = table[lo : lo + n, :]
        part_f = part.astype(f32)
        inverse_class = lax.rsqrt(jnp.sum(part_f * part_f, axis=1, keepdims=True) + 1e-06)
        scaled = lax.dot_general(part, emb[...], CROSS, preferred_element_type=f32) * inverse_class
        match = lax.broadcasted_iota(i32, (n, rows), 0) + lo == near
        given = given + jnp.sum(jnp.where(match, scaled, 0.0), axis=0, keepdims=True)
        others = jnp.maximum(others, jnp.max(jnp.where(match, -1e30, scaled), axis=0, keepdims=True))
    margin = (20.0 * (given * inverse_row - others * inverse_row)).astype(bf16).astype(f32)
    rank_hot = (lax.broadcasted_iota(i32, (spots.shape[1], rows), 0) == rank).astype(f32).astype(bf16)
    spots[...] = lax.dot_general((shard_hot * margin).astype(bf16), rank_hot, CROSS, preferred_element_type=f32)
    counts = lax.dot_general(jnp.ones((8, rows), bf16), shard_bf, CROSS, preferred_element_type=f32)[0:1]

    def fill_meta(k, c):
        a, b = place(owners, subs, k)
        meta[k, 0:1, :] = spots[pl.ds(a * subs + b, 1), :]
        meta[k, 1:2, :] = counts
        return c

    lax.fori_loop(0, shards - 1, fill_meta, 0)
    got[own, 0:1, :] = spots[pl.ds(own, 1), :]
    got[own, 1:2, :] = counts

    lax.fori_loop(early, early + 1, step, 0)

    def send_meta(k, c):
        meta_copy(k, own).start()
        return c

    lax.fori_loop(0, shards - 1, send_meta, 0)
    lax.fori_loop(early + 1, shards, step, 0)
    own_copy = pltpu.make_async_copy(send.at[shards - 1], rows_ref.at[own], own_sem)
    own_copy.start()

    def take_meta(k, c):
        source = (own + 1 + k) % shards
        meta_copy(k, source).wait_recv()
        return c

    lax.fori_loop(0, shards - 1, take_meta, 0)

    def lay(s, c):
        scores_s[pl.ds(s, 1), :] = got[s, 0:1, :]
        counts_s[pl.ds(s, 1), :] = got[s, 1:2, :]
        return c

    lax.fori_loop(0, shards, lay, 0)
    table_counts = counts_s[...]
    totals_ref[...] = jnp.sum(table_counts, axis=0, keepdims=True).astype(i32)
    below = (
        lax.broadcasted_iota(i32, (shards, shards), 1) < lax.broadcasted_iota(i32, (shards, shards), 0)
    ).astype(f32)
    before = jnp.dot(below, table_counts, preferred_element_type=f32, precision=lax.Precision.HIGHEST)
    mine = lax.broadcasted_iota(i32, (shards, wide), 1) == own
    count_col = jnp.sum(jnp.where(mine, table_counts, 0.0), axis=1, keepdims=True).astype(i32)
    before_col = jnp.sum(jnp.where(mine, before, 0.0), axis=1, keepdims=True).astype(i32)
    offset = lax.broadcasted_iota(i32, (shards, slots), 1) - cap * lax.broadcasted_iota(i32, (shards, slots), 0)
    inside = (offset >= 0) & (offset < cap)
    spot = jnp.sum(jnp.where(inside, offset, 0), axis=0, keepdims=True)
    filled = jnp.where(offset < count_col, before_col + offset, -1)
    position_ref[...] = jnp.sum(jnp.where(inside, filled, 0), axis=0, keepdims=True)
    spread = (lax.broadcasted_iota(i32, (wide, slots), 0) == spot).astype(f32).astype(bf16)
    flat = jnp.dot(scores_s[...].astype(bf16), spread, preferred_element_type=f32)
    score_ref[...] = jnp.sum(jnp.where(inside, flat, 0.0), axis=0, keepdims=True).astype(score_ref.dtype)

    def finish(k, c):
        source = (own + 1 + k) % shards
        row_copy(k, source).wait_recv()
        row_copy(k, own).wait_send()
        meta_copy(k, own).wait_send()
        return c

    lax.fori_loop(0, shards - 1, finish, 0)
    own_copy.wait()


def quick_kernel(groups, owners, subs, cap, base, depth, near_hbm, keep_hbm, dest_hbm, emb_hbm, table_hbm,
                 rows_ref, score_ref, position_ref, totals_ref, flag_ref,
                 near_ref, keep_ref, dest_ref, emb, table, keep2, earlier, send, spare, spill, news, heard, told, scored,
                 heard_s, scores_s, slot_s, verdict,
                 in_sem, send_sem, recv_sem, news_send, news_recv, score_send, score_recv, spare_send, spare_recv,
                 relay_send, relay_recv, flag_send, flag_recv, own_sem):
    f32, bf16, i32 = jnp.float32, jnp.bfloat16, jnp.int32
    shards = owners * subs
    rows, width = emb.shape
    classes = table.shape[0]
    wide = news.shape[2]
    lead = wide - shards
    slots = shards * cap
    g, o, z = lax.axis_index("groups"), lax.axis_index("owners"), lax.axis_index("sub")
    own = o * subs + z
    peers = [(o + 1 + i) % owners for i in range(owners)]
    planes = [place(owners, subs, j * owners)[1] for j in range(subs)]

    small = [
        pltpu.make_async_copy(near_hbm, near_ref, in_sem.at[2]),
        pltpu.make_async_copy(keep_hbm, keep_ref, in_sem.at[3]),
        pltpu.make_async_copy(dest_hbm, dest_ref, in_sem.at[4]),
    ]
    for copy in small:
        copy.start()
    emb_copy = pltpu.make_async_copy(emb_hbm, emb, in_sem.at[0])
    emb_copy.start()
    table_copy = pltpu.make_async_copy(table_hbm, table, in_sem.at[1])
    table_copy.start()

    def device(j, i):
        return {"owners": peers[i], "sub": planes[j]}

    pairs = [(j, i) for j in range(subs) for i in range(owners)][: shards - 1]
    barrier = pltpu.get_barrier_semaphore()
    for j, i in pairs:
        pl.semaphore_signal(barrier, inc=1, device_id=device(j, i), device_id_type=MESH)
    for i in range(1, groups):
        pl.semaphore_signal(barrier, inc=1, device_id={"groups": (g + i) % groups}, device_id_type=MESH)

    earlier[...] = (
        lax.broadcasted_iota(i32, (rows, rows), 0) < lax.broadcasted_iota(i32, (rows, rows), 1)
    ).astype(f32).astype(bf16)
    keep2[...] = jnp.zeros_like(keep2)
    for copy in small:
        copy.wait()
    near = near_ref[...]
    target = dest_ref[...]
    for h in range(up(classes, 128) // 128):
        n = min(128, classes - h * 128)
        keep2[h : h + 1, :n] = keep_ref[:, h * 128 : h * 128 + n].astype(f32)
    deep = keep2.shape[0]
    high = near // 128
    low = near - high * 128
    low_hot = (lax.broadcasted_iota(i32, (128, rows), 0) == low).astype(f32).astype(bf16)
    by_high = jnp.dot(keep2[...].astype(bf16), low_hot, preferred_element_type=f32)
    kept = jnp.sum(
        jnp.where(lax.broadcasted_iota(i32, (deep, rows), 0) == high, by_high, 0.0), axis=0, keepdims=True
    )
    shard_hot = jnp.where(lax.broadcasted_iota(i32, (up(shards, 8), rows), 0) == target, kept, 0.0)
    running = jnp.dot(shard_hot.astype(bf16), earlier[...], preferred_element_type=f32)
    rank = jnp.sum(shard_hot * running, axis=0, keepdims=True).astype(i32)
    slot_s[...] = jnp.where(kept > 0.5, target * cap + rank, -1)

    ahead = target - target // subs * subs - z
    ahead = jnp.where(ahead < 0, ahead + subs, ahead)
    over = (kept > 0.5) & (rank >= base) & (ahead > 0)
    plane_hot = jnp.where((lax.broadcasted_iota(i32, (up(subs, 8), rows), 0) == ahead) & over, 1.0, 0.0)
    before_it = jnp.dot(plane_hot.astype(bf16), earlier[...], preferred_element_type=f32)
    spot = jnp.sum(plane_hot * before_it, axis=0, keepdims=True).astype(i32)
    fits = over & (spot < depth)
    nth = jnp.where(fits, spot + 1, 0).astype(f32)

    rank_hot = (lax.broadcasted_iota(i32, (wide, rows), 0) == rank).astype(f32).astype(bf16)
    count_hot = jnp.where(lax.broadcasted_iota(i32, (wide, rows), 0) == target + lead, kept, 0.0).astype(bf16)
    notes = lax.dot_general((shard_hot * nth).astype(bf16), rank_hot, CROSS, preferred_element_type=f32)
    notes = notes + lax.dot_general(
        jnp.ones((up(shards, 8), rows), bf16), count_hot, CROSS, preferred_element_type=f32
    )
    for t in range(shards):
        news[t] = notes[t : t + 1]
    heard[own] = news[own]

    emb_copy.wait()

    seat = jnp.where(fits, (ahead - 1) * depth + spot, -1)
    hot = (lax.broadcasted_iota(i32, ((subs - 1) * depth, rows), 0) == seat).astype(f32).astype(bf16)
    packed = jnp.dot(hot, emb[...], preferred_element_type=f32).astype(bf16)
    for d in range(subs - 1):
        spare[d] = packed[d * depth : (d + 1) * depth]

    def fill(j, n):
        slot = slot_s[...] - planes[j] * cap
        hot = jnp.concatenate([
            (slot - a * subs * cap == lax.broadcasted_iota(i32, (n, rows), 0)).astype(f32).astype(bf16) for a in peers
        ])
        block = jnp.dot(hot, emb[...], preferred_element_type=f32).astype(bf16)
        for i in range(owners):
            send[j * owners + i, :n] = block[i * n : (i + 1) * n]

    def row_copy(j, i, n):
        k = j * owners + i
        return pltpu.make_async_remote_copy(
            src_ref=send.at[k, :n], dst_ref=rows_ref.at[own, :n],
            send_sem=send_sem.at[k], recv_sem=recv_sem.at[own],
            device_id=device(j, i), device_id_type=MESH,
        )

    def row_arrival(j, i, n):
        source = peers[i] * subs + planes[j]
        return pltpu.make_async_remote_copy(
            src_ref=send.at[0, :n], dst_ref=rows_ref.at[source, :n],
            send_sem=send_sem.at[0], recv_sem=recv_sem.at[source],
            device_id=device(j, i), device_id_type=MESH,
        )

    def note_copy(j, i, ref, landing, out_sem, in_sem, source):
        t = peers[i] * subs + planes[j]
        return pltpu.make_async_remote_copy(
            src_ref=ref.at[t], dst_ref=landing.at[source],
            send_sem=out_sem.at[t], recv_sem=in_sem.at[source],
            device_id=device(j, i), device_id_type=MESH,
        )

    def news_copy(j, i, source):
        return note_copy(j, i, news, heard, news_send, news_recv, source)

    def score_copy(j, i, source):
        return note_copy(j, i, told, scored, score_send, score_recv, source)

    ways = [(b - z + subs) % subs for b in planes[: subs - 1]]

    def spare_copy(j, arrival=False):
        slot = ways[j] - 1 if arrival else subs - 1 - ways[j]
        return pltpu.make_async_remote_copy(
            src_ref=spare.at[ways[j] - 1], dst_ref=spill.at[o, slot],
            send_sem=spare_send.at[ways[j] - 1], recv_sem=spare_recv.at[slot],
            device_id={"owners": o, "sub": planes[j]}, device_id_type=MESH,
        )

    def relay_copy(i, j, source):
        slot = ways[j] - 1
        return pltpu.make_async_remote_copy(
            src_ref=spill.at[source, slot], dst_ref=spill.at[source, slot],
            send_sem=relay_send.at[i, slot], recv_sem=relay_recv.at[source, slot],
            device_id={"owners": peers[i], "sub": z}, device_id_type=MESH,
        )

    def flag_copy(i, source):
        return pltpu.make_async_remote_copy(
            src_ref=verdict.at[g], dst_ref=verdict.at[source],
            send_sem=flag_send.at[i], recv_sem=flag_recv.at[source],
            device_id={"groups": (g + i) % groups}, device_id_type=MESH,
        )

    pl.semaphore_wait(barrier, shards - 1 + groups - 1)
    for j in range(subs - 1):
        spare_copy(j).start()
    for j, i in pairs:
        news_copy(j, i, own).start()
    fill(0, base)
    for i in range(owners):
        row_copy(0, i, base).start()
    fill(subs - 1, cap)
    for i in range(owners - 1):
        row_copy(subs - 1, i, cap).start()
    own_copy = pltpu.make_async_copy(send.at[shards - 1], rows_ref.at[own], own_sem)
    own_copy.start()
    square = emb[...].astype(f32)
    square = square * square
    square_hi = square.astype(bf16)
    square_lo = (square - square_hi.astype(f32)).astype(bf16)
    ones = jnp.ones((8, width), bf16)
    total = lax.dot_general(ones, square_hi, CROSS, preferred_element_type=f32)
    total = total + lax.dot_general(ones, square_lo, CROSS, preferred_element_type=f32)
    inverse_row = lax.rsqrt(total[0:1] + 1e-06)
    table_copy.wait()
    given = jnp.zeros((1, rows), f32)
    others = jnp.full((1, rows), -1e30, f32)
    for lo in range(0, classes, 128):
        n = min(128, classes - lo)
        part = table[lo : lo + n, :]
        part_f = part.astype(f32)
        inverse_class = lax.rsqrt(jnp.sum(part_f * part_f, axis=1, keepdims=True) + 1e-06)
        scaled = lax.dot_general(part, emb[...], CROSS, preferred_element_type=f32) * inverse_class
        match = lax.broadcasted_iota(i32, (n, rows), 0) + lo == near
        given = given + jnp.sum(jnp.where(match, scaled, 0.0), axis=0, keepdims=True)
        others = jnp.maximum(others, jnp.max(jnp.where(match, -1e30, scaled), axis=0, keepdims=True))
    margin = (20.0 * (given * inverse_row - others * inverse_row)).astype(bf16).astype(f32)
    rank_hot = (lax.broadcasted_iota(i32, (wide, rows), 0) == rank).astype(f32).astype(bf16)
    marks = lax.dot_general((shard_hot * margin).astype(bf16), rank_hot, CROSS, preferred_element_type=f32)
    for t in range(shards):
        told[t] = marks[t : t + 1]
    scored[own] = told[own]
    fill(1, base)
    for j, i in pairs:
        score_copy(j, i, own).start()
    for j in range(1, subs - 1):
        if j > 1:
            fill(j, base)
        for i in range(owners):
            row_copy(j, i, base).start()

    for j, i in pairs:
        news_copy(j, i, peers[i] * subs + planes[j]).wait_recv()
    for t in range(shards):
        heard_s[t : t + 1, :] = heard[t]
    counts = jnp.where(lax.broadcasted_iota(i32, (shards, wide), 1) >= lead, heard_s[...], 0.0)
    row_i, col_i = lax.broadcasted_iota(i32, (wide, wide), 0), lax.broadcasted_iota(i32, (wide, wide), 1)
    plane = ((row_i >= lead) & ((row_i - lead) % subs == col_i)).astype(f32)
    past = jnp.dot(jnp.maximum(counts - base, 0.0), plane, preferred_element_type=f32)
    away = lax.broadcasted_iota(i32, (shards, wide), 0) % subs != lax.broadcasted_iota(i32, (shards, wide), 1)
    most = jnp.max(jnp.max(jnp.where(away, past, 0.0), axis=1, keepdims=True), axis=0, keepdims=True)
    verdict[g] = jnp.broadcast_to(most, (1, wide))

    totals_ref[...] = jnp.sum(counts, axis=0, keepdims=True)[:, lead:].astype(i32)
    below = (
        lax.broadcasted_iota(i32, (shards, shards), 1) < lax.broadcasted_iota(i32, (shards, shards), 0)
    ).astype(f32)
    before = jnp.dot(below, counts, preferred_element_type=f32, precision=lax.Precision.HIGHEST)
    mine = lax.broadcasted_iota(i32, (shards, wide), 1) == own + lead
    count_col = jnp.sum(jnp.where(mine, counts, 0.0), axis=1, keepdims=True).astype(i32)
    before_col = jnp.sum(jnp.where(mine, before, 0.0), axis=1, keepdims=True).astype(i32)
    for i in range(1, groups):
        flag_copy(i, g).start()
    offset = lax.broadcasted_iota(i32, (shards, slots), 1) - cap * lax.broadcasted_iota(i32, (shards, slots), 0)
    inside = (offset >= 0) & (offset < cap)
    nook = jnp.sum(jnp.where(inside, offset, 0), axis=0, keepdims=True)
    filled = jnp.where(offset < count_col, before_col + offset, -1)
    position_ref[...] = jnp.sum(jnp.where(inside, filled, 0), axis=0, keepdims=True)

    def merge(a, j):
        s = a * subs + planes[j]
        nth_row = heard[s][:, base:cap].astype(i32)
        pick = (lax.broadcasted_iota(i32, (depth, cap - base), 0) + 1 == nth_row).astype(f32).astype(bf16)
        rest = lax.dot_general(pick, spill[a, ways[j] - 1], DOWN, preferred_element_type=f32)
        rows_ref[s, base:cap] = rest.astype(bf16)

    order = [*range(1, subs - 1), 0]
    for j in order:
        spare_copy(j, True).wait_recv()
        for i in range(owners - 1):
            relay_copy(i, j, o).start()
        merge(o, j)
    for i in range(1, groups):
        flag_copy(i, (g + groups - i) % groups).wait_recv()
    flag_ref[0] = (jnp.max(verdict[...]) > depth).astype(i32)
    for j in order:
        for i in range(owners - 1):
            relay_copy(i, j, peers[i]).wait_recv()
            merge(peers[i], j)

    for j, i in pairs:
        score_copy(j, i, peers[i] * subs + planes[j]).wait_recv()
    for t in range(shards):
        scores_s[t : t + 1, :] = scored[t]
    spread = (lax.broadcasted_iota(i32, (wide, slots), 0) == nook).astype(f32).astype(bf16)
    flat = jnp.dot(scores_s[...].astype(bf16), spread, preferred_element_type=f32)
    score_ref[...] = jnp.sum(jnp.where(inside, flat, 0.0), axis=0, keepdims=True).astype(score_ref.dtype)

    for i in range(1, groups):
        flag_copy(i, g).wait_send()
    for j in range(subs - 1):
        spare_copy(j).wait_send()
    for j in range(subs - 1):
        for i in range(owners - 1):
            relay_copy(i, j, o).wait_send()
    own_copy.wait()
    for j, i in pairs:
        news_copy(j, i, own).wait_send()
        score_copy(j, i, own).wait_send()
        row_copy(j, i, base if j < subs - 1 else cap).wait_send()
    for j, i in pairs:
        row_arrival(j, i, base if j < subs - 1 else cap).wait_recv()


def plain(call, embeddings, class_table, nearest, keep_class, destination):
    owners, subs = lax.axis_size("owners"), lax.axis_size("sub")
    shards = owners * subs
    rows, width = embeddings.shape
    classes = class_table.shape[0]
    cap = 3 * rows // (2 * shards)
    wide = up(max(shards, cap), 128)
    early = max(2, shards // 4)
    vmem = pl.BlockSpec(memory_space=pltpu.VMEM)
    hbm = pl.BlockSpec(memory_space=pl.ANY)
    f32, bf16, i32 = jnp.float32, jnp.bfloat16, jnp.int32
    dma = pltpu.SemaphoreType.DMA
    return pl.pallas_call(
        functools.partial(kernel, owners, subs, cap, early),
        out_shape=(
            pltpu.VMEM((shards, cap, width), bf16),
            pltpu.VMEM((1, shards * cap), f32),
            pltpu.VMEM((1, shards * cap), i32),
            pltpu.VMEM((1, wide), i32),
        ),
        in_specs=[hbm] * 5,
        out_specs=(vmem,) * 4,
        scratch_shapes=[
            pltpu.VMEM((1, rows), i32),
            pltpu.VMEM((1, classes), i32),
            pltpu.VMEM((1, rows), i32),
            pltpu.VMEM((rows, width), bf16),
            pltpu.VMEM((classes, width), bf16),
            pltpu.VMEM((up(up(classes, 128) // 128, 8), 128), f32),
            pltpu.VMEM((shards, cap, width), bf16),
            pltpu.VMEM((shards, 2, wide), f32),
            pltpu.VMEM((shards, 2, wide), f32),
            pltpu.VMEM((wide, wide), f32),
            pltpu.VMEM((shards, wide), f32),
            pltpu.VMEM((shards, wide), f32),
            pltpu.VMEM((1, rows), i32),
            dma((5,)),
            dma((shards,)),
            dma((shards,)),
            dma((shards,)),
            dma((shards,)),
            dma,
        ],
        compiler_params=pltpu.CompilerParams(collective_id=call, has_side_effects=True),
    )(
        nearest.reshape(1, rows),
        keep_class.reshape(1, classes),
        destination.reshape(1, rows),
        embeddings,
        class_table,
    )


def quick(base, depth, embeddings, class_table, nearest, keep_class, destination):
    groups, owners, subs = lax.axis_size("groups"), lax.axis_size("owners"), lax.axis_size("sub")
    shards = owners * subs
    rows, width = embeddings.shape
    classes = class_table.shape[0]
    cap = 3 * rows // (2 * shards)
    wide = up(shards + cap, 128)
    vmem = pl.BlockSpec(memory_space=pltpu.VMEM)
    hbm = pl.BlockSpec(memory_space=pl.ANY)
    f32, bf16, i32 = jnp.float32, jnp.bfloat16, jnp.int32
    dma = pltpu.SemaphoreType.DMA
    return pl.pallas_call(
        functools.partial(quick_kernel, groups, owners, subs, cap, base, depth),
        out_shape=(
            pltpu.VMEM((shards, cap, width), bf16),
            pltpu.VMEM((1, shards * cap), f32),
            pltpu.VMEM((1, shards * cap), i32),
            pltpu.VMEM((1, shards), i32),
            pltpu.SMEM((1,), i32),
        ),
        in_specs=[hbm] * 5,
        out_specs=(vmem,) * 4 + (pl.BlockSpec(memory_space=pltpu.SMEM),),
        scratch_shapes=[
            pltpu.VMEM((1, rows), i32),
            pltpu.VMEM((1, classes), i32),
            pltpu.VMEM((1, rows), i32),
            pltpu.VMEM((rows, width), bf16),
            pltpu.VMEM((classes, width), bf16),
            pltpu.VMEM((up(up(classes, 128) // 128, 8), 128), f32),
            pltpu.VMEM((rows, rows), bf16),
            pltpu.VMEM((shards, cap, width), bf16),
            pltpu.VMEM((subs - 1, depth, width), bf16),
            pltpu.VMEM((owners, subs - 1, depth, width), bf16),
            pltpu.VMEM((shards, 1, wide), f32),
            pltpu.VMEM((shards, 1, wide), f32),
            pltpu.VMEM((shards, 1, wide), f32),
            pltpu.VMEM((shards, 1, wide), f32),
            pltpu.VMEM((shards, wide), f32),
            pltpu.VMEM((shards, wide), f32),
            pltpu.VMEM((1, rows), i32),
            pltpu.VMEM((groups, 1, wide), f32),
            dma((5,)),
            dma((shards,)),
            dma((shards,)),
            dma((shards,)),
            dma((shards,)),
            dma((shards,)),
            dma((shards,)),
            dma((subs - 1,)),
            dma((subs - 1,)),
            dma((owners, subs - 1)),
            dma((owners, subs - 1)),
            dma((groups,)),
            dma((groups,)),
            dma,
        ],
        compiler_params=pltpu.CompilerParams(collective_id=0, has_side_effects=True),
    )(
        nearest.reshape(1, rows),
        keep_class.reshape(1, classes),
        destination.reshape(1, rows),
        embeddings,
        class_table,
    )


def close(got_rows, score, position, totals):
    shards, cap, width = got_rows.shape
    wide = totals.shape[1]
    vmem = pl.BlockSpec(memory_space=pltpu.VMEM)
    hbm = pl.BlockSpec(memory_space=pl.ANY)
    bf16, i32 = jnp.bfloat16, jnp.int32
    dma = pltpu.SemaphoreType.DMA
    small = [pltpu.with_memory_space_constraint(x, pltpu.VMEM) for x in (got_rows, score, position, totals)]
    rows_out, score_out, position_out, totals_out = pl.pallas_call(
        finish_kernel,
        out_shape=(
            jax.ShapeDtypeStruct((shards, cap, width), bf16),
            jax.ShapeDtypeStruct((shards * cap,), bf16),
            jax.ShapeDtypeStruct((shards * cap,), i32),
            jax.ShapeDtypeStruct((wide,), i32),
        ),
        in_specs=[vmem] * 4,
        out_specs=(hbm,) * 4,
        scratch_shapes=[
            pltpu.VMEM((shards * cap,), bf16),
            pltpu.VMEM((shards * cap,), i32),
            pltpu.VMEM((wide,), i32),
            dma((4,)),
        ],
    )(*small)
    return rows_out.reshape(shards * cap, width), score_out, position_out, totals_out[:shards]


def on_device(*args):
    rows = args[0].shape[0]
    subs, shards = lax.axis_size("sub"), lax.axis_size("owners") * lax.axis_size("sub")
    cap = 3 * rows // (2 * shards)
    base, depth = 2 * cap // 3, cap // 2
    if subs < 2 or shards % 8 or base % 16 or cap % 16 or depth % 8:
        return close(*plain(0, *args))
    *packed, flag = quick(base, depth, *args)

    def fast(inputs, results):
        return close(*results)

    def slow(inputs, results):
        return close(*plain(1, *inputs))

    return lax.cond(flag.reshape(()) > 0, slow, fast, args, tuple(packed))


def solution(mesh):
    in_specs = (
        P(("groups", "owners", "sub"), None),
        P(),
        P(("groups", "owners", "sub")),
        P(),
        P(("groups", "owners", "sub"), None),
    )
    out_specs = (
        P(("groups", "owners", "sub"), None),
        P(("groups", "owners", "sub")),
        P(("groups", "owners", "sub")),
        P("groups"),
    )
    return jax.shard_map(
        on_device, mesh=mesh, in_specs=in_specs, out_specs=out_specs, check_vma=False
    )
```

profile of v0, /device:TPU:9, one launch (start us, length us, event | category | flops | bytes accessed | tf_op | source)
XLA Modules:
  0.0 29.5 jit_solution(5811094129263811416)
XLA Ops:
  0.6 0.0 copy-start.4
  0.6 0.0 copy-start.2
  0.7 0.0 copy-start.3
  0.7 0.0 copy-start
  0.7 0.0 copy-start.1
  0.7 27.7 %shard_map.84 = (bf16[16,48,768]{2,1,0:T(8,128)(2,1)S(1)}, f32[1,768]{1,0:T(1,128)S(1)}, s32[1,768]{1,0:T(1,128)S(1)}, s32[1,16]{1,0:T(1,128)S(1)}, s32[1]{0:T(128)S(4)}) custom-call(s32[1,512]{1,0:T(1,128)} %bitcast.11, s32[1,1000]{1,0:T(1,128)} %bitcast.9, s32[1,512]{1,0:T(1,128)} %bitcast.13, bf16[512,768]{1,0:T(8,128)(2,1)} %emb_hbm.1, ...), custom_call_target="tpu_custom_call" | custom-call | tf_op jit(solution)/shard_map/pallas_call | solution.py:568
  28.4 0.0 copy-done.4
  28.4 0.0 copy-done.2
  28.4 0.0 copy-done.3
  28.4 0.0 copy-done
  28.4 0.0 copy-done.1
  28.4 1.1 %conditional.1 = (bf16[768]{0:T(1024)(128)(2,1)}, s32[768]{0:T(1024)}, s32[16]{0:T(128)}, bf16[16,48,768]{2,1,0:T(8,128)(2,1)}) conditional(s32[]{:T(128)} %bitcast.6, (bf16[16,48,768]{2,1,0:T(8,128)(2,1)S(1)}, f32[1,768]{1,0:T(1,128)S(1)}, s32[1,768]{1,0:T(1,128)S(1)}, s32[1,16]{1,0:T(1,128)S(1)}) %tuple.15, (s32[512]{0:T(512)S(1)}, ...), branch_computations={%region_0.0_spmd, %region_1.0_spmd} | conditional | bytes 32 | solution.py:666
  28.4 1.1 %branch_0_fun.1 = (bf16[16,48,768]{2,1,0:T(8,128)(2,1)}, bf16[768]{0:T(1024)(128)(2,1)}, s32[768]{0:T(1024)}, s32[16]{0:T(128)}) custom-call(bf16[16,48,768]{2,1,0:T(8,128)(2,1)S(1)} %get-tuple-element.18.rows_ref, f32[1,768]{1,0:T(1,128)S(1)} %get-tuple-element.19.score_ref, s32[1,768]{1,0:T(1,128)S(1)} %get-tuple-element.20.position_ref, ...), custom_call_target="tpu_custom_call" | custom-call | tf_op jit(solution)/shard_map/cond/branch_0_fun/pallas_call | solution.py:631
Async XLA Ops:
  0.6 27.7 %copy-start.4 = (s32[512,1]{0,1:T(1,128)S(1)}, s32[512,1]{0,1:T(1,128)}, u32[]{:S(2)}) copy-start(s32[512,1]{0,1:T(1,128)} %param.11) | copy-start | bytes 6148
  0.6 27.7 %copy-start.2 = (s32[1000]{0:T(1024)S(1)}, s32[1000]{0:T(1024)}, u32[]{:S(2)}) copy-start(s32[1000]{0:T(1024)} %param.10) | copy-start | bytes 12004
  0.7 27.7 %copy-start.3 = (s32[512]{0:T(512)S(1)}, s32[512]{0:T(512)}, u32[]{:S(2)}) copy-start(s32[512]{0:T(512)} %param.9) | copy-start | bytes 6148
  0.7 27.7 %copy-start = (bf16[1000,768]{1,0:T(8,128)(2,1)S(1)}, bf16[1000,768]{1,0:T(8,128)(2,1)}, u32[]{:S(2)}) copy-start(bf16[1000,768]{1,0:T(8,128)(2,1)} %table_hbm.1) | copy-start | bytes 4608004
  0.7 27.7 %copy-start.1 = (bf16[512,768]{1,0:T(8,128)(2,1)S(1)}, bf16[512,768]{1,0:T(8,128)(2,1)}, u32[]{:S(2)}) copy-start(bf16[512,768]{1,0:T(8,128)(2,1)} %emb_hbm.1) | copy-start | bytes 2359300
where the time goes:
time: 29.7 us; the launch traced here: 29.5 us
  Pallas kernels  28.7 us (97%)
  between operations  0.72 us (2%)
    pallas_call x1, Pallas kernels, quick(): pl.pallas_call(functools.partial(quick_kernel, groups, owners, subs, cap,...  27.7 us
    pallas_call x1, Pallas kernels, close(): pl.pallas_call(finish_kernel, out_shape=(jax.ShapeDtypeStruct((shards, ca...  1.06 us

commit v1 on v0

--- a/solution.py
+++ b/solution.py
@@ -427,6 +427,11 @@
             fill(j, base)
         for i in range(owners):
             row_copy(j, i, base).start()
+    order = [*range(1, subs - 1), 0]
+    for j in order:
+        spare_copy(j, True).wait_recv()
+        for i in range(owners - 1):
+            relay_copy(i, j, o).start()
 
     for j, i in pairs:
         news_copy(j, i, peers[i] * subs + planes[j]).wait_recv()
@@ -463,11 +468,7 @@
         rest = lax.dot_general(pick, spill[a, ways[j] - 1], DOWN, preferred_element_type=f32)
         rows_ref[s, base:cap] = rest.astype(bf16)
 
-    order = [*range(1, subs - 1), 0]
     for j in order:
-        spare_copy(j, True).wait_recv()
-        for i in range(owners - 1):
-            relay_copy(i, j, o).start()
         merge(o, j)
     for i in range(1, groups):
         flag_copy(i, (g + groups - i) % groups).wait_recv()

time: 29.7 us -> 28.9 us (0.973)
  Pallas kernels: 28.7 us -> 27.9 us
    pallas_call x1, Pallas kernels: 27.7 us -> 26.9 us  [quick(): pl.pallas_call(functools.partial(quick_kernel, groups, owners, subs, cap,...]
where the time goes in v1:
time: 28.9 us; the launch traced here: 28.7 us
  Pallas kernels  27.9 us (97%)
  between operations  0.72 us (2%)
    pallas_call x1, Pallas kernels, quick(): pl.pallas_call(functools.partial(quick_kernel, groups, owners, subs, cap,...  26.9 us
    pallas_call x1, Pallas kernels, close(): pl.pallas_call(finish_kernel, out_shape=(jax.ShapeDtypeStruct((shards, ca...  1.06 us

profile of v1, /device:TPU:9, one launch (start us, length us, event | category | flops | bytes accessed | tf_op | source)
XLA Modules:
  0.0 28.7 jit_solution(8014500019449029757)
XLA Ops:
  0.6 0.0 copy-start.4
  0.6 0.0 copy-start.2
  0.7 0.0 copy-start.3
  0.7 0.0 copy-start
  0.7 0.0 copy-start.1
  0.7 26.9 %shard_map.84 = (bf16[16,48,768]{2,1,0:T(8,128)(2,1)S(1)}, f32[1,768]{1,0:T(1,128)S(1)}, s32[1,768]{1,0:T(1,128)S(1)}, s32[1,16]{1,0:T(1,128)S(1)}, s32[1]{0:T(128)S(4)}) custom-call(s32[1,512]{1,0:T(1,128)} %bitcast.11, s32[1,1000]{1,0:T(1,128)} %bitcast.9, s32[1,512]{1,0:T(1,128)} %bitcast.13, bf16[512,768]{1,0:T(8,128)(2,1)} %emb_hbm.1, ...), custom_call_target="tpu_custom_call" | custom-call | tf_op jit(solution)/shard_map/pallas_call | solution.py:569
  27.6 0.0 copy-done.4
  27.6 0.0 copy-done.2
  27.6 0.0 copy-done.3
  27.6 0.0 copy-done
  27.6 0.0 copy-done.1
  27.6 1.1 %conditional.1 = (bf16[768]{0:T(1024)(128)(2,1)}, s32[768]{0:T(1024)}, s32[16]{0:T(128)}, bf16[16,48,768]{2,1,0:T(8,128)(2,1)}) conditional(s32[]{:T(128)} %bitcast.6, (bf16[16,48,768]{2,1,0:T(8,128)(2,1)S(1)}, f32[1,768]{1,0:T(1,128)S(1)}, s32[1,768]{1,0:T(1,128)S(1)}, s32[1,16]{1,0:T(1,128)S(1)}) %tuple.15, (s32[512]{0:T(512)S(1)}, ...), branch_computations={%region_0.0_spmd, %region_1.0_spmd} | conditional | bytes 32 | solution.py:667
  27.6 1.1 %branch_0_fun.1 = (bf16[16,48,768]{2,1,0:T(8,128)(2,1)}, bf16[768]{0:T(1024)(128)(2,1)}, s32[768]{0:T(1024)}, s32[16]{0:T(128)}) custom-call(bf16[16,48,768]{2,1,0:T(8,128)(2,1)S(1)} %get-tuple-element.18.rows_ref, f32[1,768]{1,0:T(1,128)S(1)} %get-tuple-element.19.score_ref, s32[1,768]{1,0:T(1,128)S(1)} %get-tuple-element.20.position_ref, ...), custom_call_target="tpu_custom_call" | custom-call | tf_op jit(solution)/shard_map/cond/branch_0_fun/pallas_call | solution.py:632
Async XLA Ops:
  0.6 26.9 %copy-start.4 = (s32[512,1]{0,1:T(1,128)S(1)}, s32[512,1]{0,1:T(1,128)}, u32[]{:S(2)}) copy-start(s32[512,1]{0,1:T(1,128)} %param.11) | copy-start | bytes 6148
  0.6 26.9 %copy-start.2 = (s32[1000]{0:T(1024)S(1)}, s32[1000]{0:T(1024)}, u32[]{:S(2)}) copy-start(s32[1000]{0:T(1024)} %param.10) | copy-start | bytes 12004
  0.7 26.9 %copy-start.3 = (s32[512]{0:T(512)S(1)}, s32[512]{0:T(512)}, u32[]{:S(2)}) copy-start(s32[512]{0:T(512)} %param.9) | copy-start | bytes 6148
  0.7 26.9 %copy-start = (bf16[1000,768]{1,0:T(8,128)(2,1)S(1)}, bf16[1000,768]{1,0:T(8,128)(2,1)}, u32[]{:S(2)}) copy-start(bf16[1000,768]{1,0:T(8,128)(2,1)} %table_hbm.1) | copy-start | bytes 4608004
  0.7 26.9 %copy-start.1 = (bf16[512,768]{1,0:T(8,128)(2,1)S(1)}, bf16[512,768]{1,0:T(8,128)(2,1)}, u32[]{:S(2)}) copy-start(bf16[512,768]{1,0:T(8,128)(2,1)} %emb_hbm.1) | copy-start | bytes 2359300

commit v2 on v1

--- a/solution.py
+++ b/solution.py
@@ -230,7 +230,7 @@
                  near_ref, keep_ref, dest_ref, emb, table, keep2, earlier, send, spare, spill, news, heard, told, scored,
                  heard_s, scores_s, slot_s, verdict,
                  in_sem, send_sem, recv_sem, news_send, news_recv, score_send, score_recv, spare_send, spare_recv,
-                 relay_send, relay_recv, flag_send, flag_recv, own_sem):
+                 relay_send, relay_recv, flag_send, flag_recv, own_sem, mutual):
     f32, bf16, i32 = jnp.float32, jnp.bfloat16, jnp.int32
     shards = owners * subs
     rows, width = emb.shape
@@ -259,9 +259,14 @@
         return {"owners": peers[i], "sub": planes[j]}
 
     pairs = [(j, i) for j in range(subs) for i in range(owners)][: shards - 1]
+    half = subs // 2
+    upper = (2 * z) // subs
+    cross = [(1 - upper) * (subs - 1 - m) + upper * m for m in range(half)]
+    mates = [upper * half + (z - upper * half + m) % half for m in range(1, half)]
     barrier = pltpu.get_barrier_semaphore()
-    for j, i in pairs:
-        pl.semaphore_signal(barrier, inc=1, device_id=device(j, i), device_id_type=MESH)
+    for b in cross:
+        for a in peers:
+            pl.semaphore_signal(barrier, inc=1, device_id={"owners": a, "sub": b}, device_id_type=MESH)
     for i in range(1, groups):
         pl.semaphore_signal(barrier, inc=1, device_id={"groups": (g + i) % groups}, device_id_type=MESH)
 
@@ -341,28 +346,29 @@
             device_id=device(j, i), device_id_type=MESH,
         )
 
-    def note_copy(j, i, ref, landing, out_sem, in_sem, source):
-        t = peers[i] * subs + planes[j]
+    def note_copy(a, b, ref, landing, out_sem, in_sem, source):
+        t = a * subs + b
         return pltpu.make_async_remote_copy(
             src_ref=ref.at[t], dst_ref=landing.at[source],
             send_sem=out_sem.at[t], recv_sem=in_sem.at[source],
-            device_id=device(j, i), device_id_type=MESH,
+            device_id={"owners": a, "sub": b}, device_id_type=MESH,
         )
 
-    def news_copy(j, i, source):
-        return note_copy(j, i, news, heard, news_send, news_recv, source)
+    def news_copy(a, b, source):
+        return note_copy(a, b, news, heard, news_send, news_recv, source)
 
     def score_copy(j, i, source):
-        return note_copy(j, i, told, scored, score_send, score_recv, source)
+        return note_copy(peers[i], planes[j], told, scored, score_send, score_recv, source)
 
     ways = [(b - z + subs) % subs for b in planes[: subs - 1]]
 
-    def spare_copy(j, arrival=False):
-        slot = ways[j] - 1 if arrival else subs - 1 - ways[j]
+    def spare_copy(b, arrival=False):
+        way = (b - z + subs) % subs
+        slot = way - 1 if arrival else subs - 1 - way
         return pltpu.make_async_remote_copy(
-            src_ref=spare.at[ways[j] - 1], dst_ref=spill.at[o, slot],
-            send_sem=spare_send.at[ways[j] - 1], recv_sem=spare_recv.at[slot],
-            device_id={"owners": o, "sub": planes[j]}, device_id_type=MESH,
+            src_ref=spare.at[way - 1], dst_ref=spill.at[o, slot],
+            send_sem=spare_send.at[way - 1], recv_sem=spare_recv.at[slot],
+            device_id={"owners": o, "sub": b}, device_id_type=MESH,
         )
 
     def relay_copy(i, j, source):
@@ -380,15 +386,25 @@
             device_id={"groups": (g + i) % groups}, device_id_type=MESH,
         )
 
-    pl.semaphore_wait(barrier, shards - 1 + groups - 1)
-    for j in range(subs - 1):
-        spare_copy(j).start()
-    for j, i in pairs:
-        news_copy(j, i, own).start()
+    pl.semaphore_wait(barrier, half * owners + groups - 1)
+    pl.semaphore_signal(
+        mutual, inc=1, device_id={"owners": o, "sub": (z + half) % subs}, device_id_type=MESH
+    )
+    for b in cross:
+        spare_copy(b).start()
+    for b in cross:
+        for a in peers:
+            news_copy(a, b, own).start()
     fill(0, base)
     for i in range(owners):
         row_copy(0, i, base).start()
     fill(subs - 1, cap)
+    pl.semaphore_wait(mutual, 1)
+    for b in mates:
+        spare_copy(b).start()
+    for b in [*mates, z]:
+        for a in peers[: owners - 1] if b is z else peers:
+            news_copy(a, b, own).start()
     for i in range(owners - 1):
         row_copy(subs - 1, i, cap).start()
     own_copy = pltpu.make_async_copy(send.at[shards - 1], rows_ref.at[own], own_sem)
@@ -429,12 +445,12 @@
             row_copy(j, i, base).start()
     order = [*range(1, subs - 1), 0]
     for j in order:
-        spare_copy(j, True).wait_recv()
+        spare_copy(planes[j], True).wait_recv()
         for i in range(owners - 1):
             relay_copy(i, j, o).start()
 
     for j, i in pairs:
-        news_copy(j, i, peers[i] * subs + planes[j]).wait_recv()
+        news_copy(peers[i], planes[j], peers[i] * subs + planes[j]).wait_recv()
     for t in range(shards):
         heard_s[t : t + 1, :] = heard[t]
     counts = jnp.where(lax.broadcasted_iota(i32, (shards, wide), 1) >= lead, heard_s[...], 0.0)
@@ -489,13 +505,13 @@
     for i in range(1, groups):
         flag_copy(i, g).wait_send()
     for j in range(subs - 1):
-        spare_copy(j).wait_send()
+        spare_copy(planes[j]).wait_send()
     for j in range(subs - 1):
         for i in range(owners - 1):
             relay_copy(i, j, o).wait_send()
     own_copy.wait()
     for j, i in pairs:
-        news_copy(j, i, own).wait_send()
+        news_copy(peers[i], planes[j], own).wait_send()
         score_copy(j, i, own).wait_send()
         row_copy(j, i, base if j < subs - 1 else cap).wait_send()
     for j, i in pairs:
@@ -610,6 +626,7 @@
             dma((groups,)),
             dma((groups,)),
             dma,
+            pltpu.SemaphoreType.REGULAR,
         ],
         compiler_params=pltpu.CompilerParams(collective_id=0, has_side_effects=True),
     )(
@@ -654,7 +671,7 @@
     subs, shards = lax.axis_size("sub"), lax.axis_size("owners") * lax.axis_size("sub")
     cap = 3 * rows // (2 * shards)
     base, depth = 2 * cap // 3, cap // 2
-    if subs < 2 or shards % 8 or base % 16 or cap % 16 or depth % 8:
+    if subs % 2 or shards % 8 or base % 16 or cap % 16 or depth % 8:
         return close(*plain(0, *args))
     *packed, flag = quick(base, depth, *args)
 

time: 28.9 us -> 28.6 us (0.990)
  the two profiles are of different devices: /device:TPU:9 before, /device:TPU:16 now
where the time goes in v2:
time: 28.6 us; the launch traced here: 28.5 us
  Pallas kernels  27.7 us (97%)
  between operations  0.72 us (3%)
    pallas_call x1, Pallas kernels, quick(): pl.pallas_call(functools.partial(quick_kernel, groups, owners, subs, cap,...  26.7 us
    pallas_call x1, Pallas kernels, close(): pl.pallas_call(finish_kernel, out_shape=(jax.ShapeDtypeStruct((shards, ca...  1.06 us

profile of v2, /device:TPU:16, one launch (start us, length us, event | category | flops | bytes accessed | tf_op | source)
XLA Modules:
  0.0 28.5 jit_solution(13413791405173632759)
XLA Ops:
  0.6 0.0 copy-start.4
  0.6 0.0 copy-start.2
  0.7 0.0 copy-start.3
  0.7 0.0 copy-start
  0.7 0.0 copy-start.1
  0.7 26.7 %shard_map.84 = (bf16[16,48,768]{2,1,0:T(8,128)(2,1)S(1)}, f32[1,768]{1,0:T(1,128)S(1)}, s32[1,768]{1,0:T(1,128)S(1)}, s32[1,16]{1,0:T(1,128)S(1)}, s32[1]{0:T(128)S(4)}) custom-call(s32[1,512]{1,0:T(1,128)} %bitcast.11, s32[1,1000]{1,0:T(1,128)} %bitcast.9, s32[1,512]{1,0:T(1,128)} %bitcast.13, bf16[512,768]{1,0:T(8,128)(2,1)} %emb_hbm.1, ...), custom_call_target="tpu_custom_call" | custom-call | tf_op jit(solution)/shard_map/pallas_call | solution.py:585
  27.4 0.0 copy-done.4
  27.4 0.0 copy-done.2
  27.4 0.0 copy-done.3
  27.4 0.0 copy-done
  27.4 0.0 copy-done.1
  27.4 1.1 %conditional.1 = (bf16[768]{0:T(1024)(128)(2,1)}, s32[768]{0:T(1024)}, s32[16]{0:T(128)}, bf16[16,48,768]{2,1,0:T(8,128)(2,1)}) conditional(s32[]{:T(128)} %bitcast.6, (bf16[16,48,768]{2,1,0:T(8,128)(2,1)S(1)}, f32[1,768]{1,0:T(1,128)S(1)}, s32[1,768]{1,0:T(1,128)S(1)}, s32[1,16]{1,0:T(1,128)S(1)}) %tuple.15, (s32[512]{0:T(512)S(1)}, ...), branch_computations={%region_0.0_spmd, %region_1.0_spmd} | conditional | bytes 32 | solution.py:684
  27.4 1.1 %branch_0_fun.1 = (bf16[16,48,768]{2,1,0:T(8,128)(2,1)}, bf16[768]{0:T(1024)(128)(2,1)}, s32[768]{0:T(1024)}, s32[16]{0:T(128)}) custom-call(bf16[16,48,768]{2,1,0:T(8,128)(2,1)S(1)} %get-tuple-element.18.rows_ref, f32[1,768]{1,0:T(1,128)S(1)} %get-tuple-element.19.score_ref, s32[1,768]{1,0:T(1,128)S(1)} %get-tuple-element.20.position_ref, ...), custom_call_target="tpu_custom_call" | custom-call | tf_op jit(solution)/shard_map/cond/branch_0_fun/pallas_call | solution.py:649
Async XLA Ops:
  0.6 26.7 %copy-start.4 = (s32[512,1]{0,1:T(1,128)S(1)}, s32[512,1]{0,1:T(1,128)}, u32[]{:S(2)}) copy-start(s32[512,1]{0,1:T(1,128)} %param.11) | copy-start | bytes 6148
  0.6 26.7 %copy-start.2 = (s32[1000]{0:T(1024)S(1)}, s32[1000]{0:T(1024)}, u32[]{:S(2)}) copy-start(s32[1000]{0:T(1024)} %param.10) | copy-start | bytes 12004
  0.7 26.7 %copy-start.3 = (s32[512]{0:T(512)S(1)}, s32[512]{0:T(512)}, u32[]{:S(2)}) copy-start(s32[512]{0:T(512)} %param.9) | copy-start | bytes 6148
  0.7 26.7 %copy-start = (bf16[1000,768]{1,0:T(8,128)(2,1)S(1)}, bf16[1000,768]{1,0:T(8,128)(2,1)}, u32[]{:S(2)}) copy-start(bf16[1000,768]{1,0:T(8,128)(2,1)} %table_hbm.1) | copy-start | bytes 4608004
  0.7 26.7 %copy-start.1 = (bf16[512,768]{1,0:T(8,128)(2,1)S(1)}, bf16[512,768]{1,0:T(8,128)(2,1)}, u32[]{:S(2)}) copy-start(bf16[512,768]{1,0:T(8,128)(2,1)} %emb_hbm.1) | copy-start | bytes 2359300

commit v3 on v2

--- a/solution.py
+++ b/solution.py
@@ -242,6 +242,8 @@
     own = o * subs + z
     peers = [(o + 1 + i) % owners for i in range(owners)]
     planes = [place(owners, subs, j * owners)[1] for j in range(subs)]
+    low = 1 - (2 * z) // subs
+    planes = [b + low * ((2 * b) // subs) * (subs // 2 + subs - 1 - 2 * b) for b in planes]
 
     small = [
         pltpu.make_async_copy(near_hbm, near_ref, in_sem.at[2]),

time: 28.6 us -> 28.6 us (level)
  the two profiles are of different devices: /device:TPU:16 before, /device:TPU:24 now
where the time goes in v3:
time: 28.6 us; the launch traced here: 28.4 us
  Pallas kernels  27.6 us (97%)
  between operations  0.72 us (3%)
    pallas_call x1, Pallas kernels, quick(): pl.pallas_call(functools.partial(quick_kernel, groups, owners, subs, cap,...  26.6 us
    pallas_call x1, Pallas kernels, close(): pl.pallas_call(finish_kernel, out_shape=(jax.ShapeDtypeStruct((shards, ca...  1.06 us

profile of v3, /device:TPU:24, one launch (start us, length us, event | category | flops | bytes accessed | tf_op | source)
XLA Modules:
  0.0 28.4 jit_solution(13693738327209345964)
XLA Ops:
  0.6 0.0 copy-start.4
  0.6 0.0 copy-start.2
  0.7 0.0 copy-start.3
  0.7 0.0 copy-start
  0.7 0.0 copy-start.1
  0.7 26.6 %shard_map.84 = (bf16[16,48,768]{2,1,0:T(8,128)(2,1)S(1)}, f32[1,768]{1,0:T(1,128)S(1)}, s32[1,768]{1,0:T(1,128)S(1)}, s32[1,16]{1,0:T(1,128)S(1)}, s32[1]{0:T(128)S(4)}) custom-call(s32[1,512]{1,0:T(1,128)} %bitcast.11, s32[1,1000]{1,0:T(1,128)} %bitcast.9, s32[1,512]{1,0:T(1,128)} %bitcast.13, bf16[512,768]{1,0:T(8,128)(2,1)} %emb_hbm.1, ...), custom_call_target="tpu_custom_call" | custom-call | tf_op jit(solution)/shard_map/pallas_call | solution.py:587
  27.3 0.0 copy-done.4
  27.3 0.0 copy-done.2
  27.3 0.0 copy-done.3
  27.3 0.0 copy-done
  27.3 0.0 copy-done.1
  27.3 1.1 %conditional.1 = (bf16[768]{0:T(1024)(128)(2,1)}, s32[768]{0:T(1024)}, s32[16]{0:T(128)}, bf16[16,48,768]{2,1,0:T(8,128)(2,1)}) conditional(s32[]{:T(128)} %bitcast.6, (bf16[16,48,768]{2,1,0:T(8,128)(2,1)S(1)}, f32[1,768]{1,0:T(1,128)S(1)}, s32[1,768]{1,0:T(1,128)S(1)}, s32[1,16]{1,0:T(1,128)S(1)}) %tuple.15, (s32[512]{0:T(512)S(1)}, ...), branch_computations={%region_0.0_spmd, %region_1.0_spmd} | conditional | bytes 32 | solution.py:686
  27.3 1.1 %branch_0_fun.1 = (bf16[16,48,768]{2,1,0:T(8,128)(2,1)}, bf16[768]{0:T(1024)(128)(2,1)}, s32[768]{0:T(1024)}, s32[16]{0:T(128)}) custom-call(bf16[16,48,768]{2,1,0:T(8,128)(2,1)S(1)} %get-tuple-element.18.rows_ref, f32[1,768]{1,0:T(1,128)S(1)} %get-tuple-element.19.score_ref, s32[1,768]{1,0:T(1,128)S(1)} %get-tuple-element.20.position_ref, ...), custom_call_target="tpu_custom_call" | custom-call | tf_op jit(solution)/shard_map/cond/branch_0_fun/pallas_call | solution.py:651
Async XLA Ops:
  0.6 26.6 %copy-start.4 = (s32[512,1]{0,1:T(1,128)S(1)}, s32[512,1]{0,1:T(1,128)}, u32[]{:S(2)}) copy-start(s32[512,1]{0,1:T(1,128)} %param.11) | copy-start | bytes 6148
  0.6 26.6 %copy-start.2 = (s32[1000]{0:T(1024)S(1)}, s32[1000]{0:T(1024)}, u32[]{:S(2)}) copy-start(s32[1000]{0:T(1024)} %param.10) | copy-start | bytes 12004
  0.7 26.6 %copy-start.3 = (s32[512]{0:T(512)S(1)}, s32[512]{0:T(512)}, u32[]{:S(2)}) copy-start(s32[512]{0:T(512)} %param.9) | copy-start | bytes 6148
  0.7 26.6 %copy-start = (bf16[1000,768]{1,0:T(8,128)(2,1)S(1)}, bf16[1000,768]{1,0:T(8,128)(2,1)}, u32[]{:S(2)}) copy-start(bf16[1000,768]{1,0:T(8,128)(2,1)} %table_hbm.1) | copy-start | bytes 4608004
  0.7 26.6 %copy-start.1 = (bf16[512,768]{1,0:T(8,128)(2,1)S(1)}, bf16[512,768]{1,0:T(8,128)(2,1)}, u32[]{:S(2)}) copy-start(bf16[512,768]{1,0:T(8,128)(2,1)} %emb_hbm.1) | copy-start | bytes 2359300
